TPU v7x, 16 devices: a whole 2x2x2 slice. The times are simulated.
16 devices in a mesh: col: 4 (over z, y), row: 4 (over x, core).
Axes of the slice: x: 2, y: 2, z: 2, core: 2. Of those that a mesh axis runs over, the one named last changes fastest.
Arguments:
- t_amp: float32 [256, 20736], P('row', 'col')
- d_denom: float32 [256, 20736], P('row', 'col')
- v_oovv: bfloat16 [256, 20736], P('row', 'col')
- v_vvvv: bfloat16 [20736, 20736], P('row', 'col')
- v_oooo: bfloat16 [256, 256], replicated
- w_ovov: bfloat16 [2304, 2304], P(None, 'col')
Outputs:
- output: float32 [2304, 2304], P('row', 'col')
All inputs are finite; a program needn't handle non-finite values.
Results may differ from a plain program's by a relative error of at most 0.001.
Values are sent between devices in bfloat16 or wider.
A program may use at most 1 GiB of HBM per device.

v0:
```python
import functools

import jax
import jax.numpy as jnp
from jax import lax
from jax.experimental import pallas as pl
from jax.experimental.pallas import tpu as pltpu
from jax.sharding import PartitionSpec as P

MESH = pl.DeviceIdType.MESH
scope = jax.named_scope
F32 = jnp.float32
BF16 = jnp.bfloat16

O = 16
V = 144
RB = 64
CB = 5184
AB = 36
PQ = 648
PB = 576
CW = 512
NCH = CB // CW
TW = CB - NCH * CW


def stripe(load, m, q):
    first = 1152 * m + V * q
    low = first // 128 * 128
    high = min(-(-(first + V) // 128) * 128, CB)
    return load(low, high)[:, first - low : first - low + V]


def split_cols(load, planes, m):
    for q in range(8 if m < 4 else 4):
        piece = stripe(load, m, q)
        base = RB * (8 * m + q)
        planes[0, base : base + RB, :] = piece[:, 0:128]
        planes[1, base : base + RB, 0:16] = piece[:, 128:144]


def take_j(planes, j, base, rows):
    wide = planes[0, pl.ds(base + j, rows, stride=16), :]
    rest = planes[1, pl.ds(base + j, rows, stride=16), :]
    return [wide, rest[:, 0:16]]


def pack(put, rows, wide):
    for b in range(4):
        put(rows * b, rows, slice(0, 128), wide[:, 128 * b : 128 * b + 128])
    put(4 * rows, rows // 2, slice(0, 64), wide[: rows // 2, 512:576])
    put(4 * rows, rows // 2, slice(64, 128), wide[rows // 2 :, 512:576])


def kernel(
    t_hbm, d_hbm, vo_hbm, vv_hbm, oo_hbm, w_hbm, out_ref,
    t32, d32, vo, wv, trow, tcol, tlad, planes, tm, r3, pp, pt, pr,
    dsnd, drcv, lsnd, lrcv, prel, xq, xqr, wt, oo, wblk, wf, vbuf, vtail,
    acc, d2r, xsb, xrb, acct, d2t, xst, xrt, r1,
    in_sem, v_sem, row_s, row_r, col_s, col_r, lad_s, lad_r, q_s, q_r,
    d_s, d_r, l_s, l_r, p_s, p_r, fw_s, dd_s, dd_r, xx_s, xx_r, w_s, w_r, f_s,
):
    r = lax.axis_index("row")
    c = lax.axis_index("col")
    x, k = r // 2, r % 2
    z, y = c // 2, c % 2
    r_k, r_x = 2 * x + 1 - k, 2 * (1 - x) + k
    r_d = 2 * (1 - x) + 1 - k
    c_y, c_z = 2 * z + 1 - y, 2 * (1 - z) + y
    c_d = 2 * (1 - z) + 1 - y
    col_peers = (c_y, c_z, c_d)

    def send(src, dst, ss, rs, row, col):
        return pltpu.make_async_remote_copy(
            src_ref=src, dst_ref=dst, send_sem=ss, recv_sem=rs,
            device_id={"row": row, "col": col}, device_id_type=MESH,
        )

    def load_v(n, slot):
        at = pl.multiple_of(n * CW, CW)
        return pltpu.make_async_copy(vv_hbm.at[:, pl.ds(at, CW)], vbuf.at[slot], v_sem.at[slot])

    load_t = pltpu.make_async_copy(t_hbm, t32, in_sem.at[0])
    load_d = pltpu.make_async_copy(d_hbm, d32, in_sem.at[1])
    load_vo = pltpu.make_async_copy(vo_hbm, vo, in_sem.at[2])
    load_w = pltpu.make_async_copy(w_hbm, wv, in_sem.at[3])
    load_tail = pltpu.make_async_copy(vv_hbm.at[:, pl.ds(NCH * CW, TW)], vtail, in_sem.at[4])
    load_oo = pltpu.make_async_copy(oo_hbm.at[pl.ds(pl.multiple_of(r * RB, RB), RB)], oo, in_sem.at[5])
    load_t.start()
    load_w.start()
    load_d.start()
    load_vo.start()
    load_tail.start()
    load_oo.start()
    load_v(0, 0).start()
    load_v(1, 1).start()

    barrier = pltpu.get_barrier_semaphore()
    for rr in range(4):
        for cc in range(4):
            pl.semaphore_signal(barrier, inc=1, device_id={"row": rr, "col": cc}, device_id_type=MESH)

    with scope("wait_t"):
        load_t.wait()
    for m in range(9):
        piece = t32[:, PB * m : PB * m + PB].astype(BF16)
        trow[c, :, PB * m : PB * m + PB] = piece
        tcol[r, :, PB * m : PB * m + PB] = piece
    with scope("barrier"):
        pl.semaphore_wait(barrier, 16)

    half = RB // 2
    halves = (slice(0, half), slice(half, RB))

    def row_copy(way, h):
        block, peer = ((c, c_y), (c, c_z), ((c_z, c_y), (c_y, c_z))[h])[way]
        piece = trow.at[block, halves[h]]
        return send(piece, piece, row_s.at[way, h], row_r.at[way, h], r, peer)

    row_extra = send(
        trow.at[c_y, halves[0]], trow.at[c_y, halves[0]], row_s.at[3, 0], row_r.at[2, 0], r, c_z
    )

    def row_wait(way, h):
        piece = trow.at[(c_y, c_z, c_d)[way], halves[h]]
        send(piece, piece, row_s.at[way, h], row_r.at[way, h], r, c_y).wait_recv()

    def col_piece(h):
        piece = tcol.at[r, halves[h]]
        return send(piece, piece, col_s.at[h], col_r.at[h], r_x, c)

    col_pair = send(tcol.at[r], tcol.at[r], col_s.at[2], col_r.at[2], r_k, c)
    col_relay = send(tcol.at[r_x], tcol.at[r_x], col_s.at[3], col_r.at[3], r_k, c)

    def lad_copy(slot, h):
        return send(trow.at[slot, halves[h]], tlad.at[r, halves[h]], lad_s.at[slot, h], lad_r.at[r, h], slot, c)

    def dispatch(slot, h):
        @pl.when(slot != r)
        def _():
            lad_copy(slot, h).start()

        @pl.when(slot == r)
        def _():
            tlad[r, halves[h]] = trow[slot, halves[h]]

    def lad_wait(slot, h):
        send(trow.at[0, halves[h]], tlad.at[slot, halves[h]], lad_s.at[slot, h], lad_r.at[slot, h], r, c).wait_recv()

    def lad_forward(slot, h):
        piece = tlad.at[slot, halves[h]]
        return send(piece, piece, fw_s.at[slot, h], lad_r.at[slot, h], r, c_y)

    gives = jnp.logical_and(x != z, k == y)

    def forward(h):
        @pl.when(gives)
        def _():
            for slot in (r_x, r_d):
                with scope("lad_f"):
                    lad_wait(slot, h)
                lad_forward(slot, h).start()

    @pl.when(x == z)
    def _():
        col_piece(0).start()

    for h in range(2):
        row_copy(0, h).start()
        row_copy(1, h).start()
        dispatch(c, h)
    col_pair.start()

    with scope("wait_w"):
        load_w.wait()

    def mixed(slot):
        for m in range(5):
            split_cols(lambda lo, hi: trow[slot, :, lo:hi].astype(F32), planes, m)
        for h in range(2):
            parts = []
            for j in range(8):
                parts += take_j(planes, 8 * h + j, 0, 4 * AB)
            tm[:, 1152 * h : 1152 * h + 1152] = jnp.concatenate(parts, axis=1).astype(BF16)
        block = lax.dot_general(tm[...], wv[...], (((1,), (1,)), ((), ())), preferred_element_type=F32)

        def put(at, rows, lanes, value):
            pt[slot, at : at + rows, lanes] = value

        pack(put, V, block)

    p_copy = send(pt, pr, p_s.at[0], p_r.at[0], c, r)
    p_out, p_on = [], []
    for q, slot in enumerate((c_y, c_d, c, c_z)):
        via, to, src = ((r_x, c), (c, r_x), slot) if q < 2 else ((r, c_z), (c_z, r), (c_z, c)[q - 2])
        p_out.append(send(pt.at[slot], prel.at[q], p_s.at[1 + q], p_r.at[1 + q], *via))
        p_on.append(send(prel.at[q], pr.at[src], p_s.at[5 + q], p_r.at[5 + q], *to))

    def p_start(q):
        @pl.when(x != z)
        def _():
            p_out[q].start()

    def relay(*quarters):
        for q in quarters:
            with scope("relay"):
                p_out[q].wait_recv()
            p_on[q].start()

    with scope("mixed_c"):
        mixed(c)

    with scope("row10"):
        row_wait(1, 0)

    @pl.when(x == z)
    def _():
        row_copy(2, 0).start()

    dispatch(c_z, 0)
    with scope("row00"):
        row_wait(0, 0)

    @pl.when(x == z)
    def _():
        row_extra.start()

    dispatch(c_y, 0)

    load_d.wait()
    for m in range(5):
        split_cols(lambda lo, hi: d32[:, lo:hi], planes, m)
    for cc in range(4):
        parts = []
        for j in range(4):
            parts += take_j(planes, 4 * cc + j, 0, 4 * AB)
        def put_d(at, rows, lanes, value):
            dsnd[cc, at : at + rows, lanes] = value

        pack(put_d, V, jnp.concatenate(parts, axis=1))
    drcv[c] = dsnd[c]

    with scope("row11"):
        row_wait(1, 1)
    dispatch(c_z, 1)
    with scope("row01"):
        row_wait(0, 1)
    row_copy(2, 1).start()
    dispatch(c_y, 1)
    d_copy = [
        send(dsnd.at[peer], drcv.at[c], d_s.at[q], d_r.at[q], r, peer) for q, peer in enumerate(col_peers)
    ]

    @pl.when(x == z)
    def _():
        col_piece(1).start()
        d_copy[0].start()

    p_start(2)
    forward(0)
    with scope("mixed_c_z"):
        mixed(c_z)
    p_start(3)
    with scope("mixed_c_y"):
        mixed(c_y)
    with scope("row20"):
        row_wait(2, 0)
    forward(1)
    p_start(0)
    with scope("row21"):
        row_wait(2, 1)

    @pl.when(x != z)
    def _():
        dispatch(c_d, 0)
        dispatch(c_d, 1)

    with scope("mixed_c_d"):
        mixed(c_d)
    p_start(1)

    q_copy = [send(xq, xqr.at[c], q_s.at[q], q_r.at[q], r, peer) for q, peer in enumerate(col_peers)]

    def hole_x():
        load_vo.wait()
        send(tcol.at[r_k], tcol.at[r_k], col_s.at[2], col_r.at[2], r_k, c).wait_recv()

        @pl.when(jnp.logical_and(x == z, r != c))
        def _():
            send(tcol.at[r_x], tcol.at[r_x], f_s.at[0], col_r.at[4], r_k, c).wait_recv()

        @pl.when(r != c)
        def _():
            send(tcol.at[r_d], tcol.at[r_d], col_s.at[3], col_r.at[3], r_k, c).wait_recv()

        xq[...] = lax.dot_general(
            vo[...], tcol[...].reshape(4 * RB, CB), (((1,), (1,)), ((), ())), preferred_element_type=F32
        )
        xqr[c] = xq[...]
        for copy in q_copy:
            copy.start()

    @pl.when(x != z)
    def _():
        with scope("col"):
            for h in range(2):
                piece = tcol.at[r_x, halves[h]]
                send(piece, piece, col_s.at[h], col_r.at[h], r_x, c).wait_recv()
        col_relay.start()
        with scope("hole_x"):
            hole_x()

    @pl.when(jnp.logical_not(gives))
    def _():
        for h in range(2):
            for slot in (r_x, r_d):
                with scope("lad"):
                    lad_wait(slot, h)

    for h in range(2):
        with scope("lad_k"):
            lad_wait(r_k, h)

    fwd = (
        send(tlad.at[r_d], tcol.at[r_d], f_s.at[0], col_r.at[4], r_k, c),
        send(tlad.at[r_x], tcol.at[r_x], f_s.at[1], col_r.at[3], r_k, c),
    )

    @pl.when(r == c)
    def _():
        for copy in fwd:
            copy.start()
        tcol[r_d] = tlad[r_d]
        tcol[r_x] = tlad[r_x]

    @pl.when(x == z)
    def _():
        with scope("hole_x"):
            hole_x()

        d_copy[1].start()

        @pl.when(r != c)
        def _():
            p_copy.start()

        @pl.when(r == c)
        def _():
            pr[...] = pt[...]

    def w_copy(rr):
        return send(wt.at[RB * rr : RB * rr + RB], wblk.at[r], w_s.at[rr], w_r.at[r], rr, c)

    def hole_w():
        load_oo.wait()
        for q, peer in enumerate(col_peers):
            send(xq, xqr.at[peer], q_s.at[q], q_r.at[q], r, peer).wait_recv()
        x_sum = (xqr[0] + xqr[1]) + (xqr[2] + xqr[3])
        w_hole = oo[...].astype(F32) + 0.5 * x_sum
        wt[...] = w_hole.T.astype(BF16)
        wblk[r] = wt[pl.ds(pl.multiple_of(r * RB, RB), RB), :]
        for rr in range(4):

            @pl.when(r != rr)
            def _():
                w_copy(rr).start()

    def d2_copy(n):
        return send(acc.at[n, 1 - k], d2r.at[n], dd_s.at[n], dd_r.at[n], r_k, c)

    def xx_copy(n):
        return send(xsb.at[n], xrb.at[n], xx_s.at[n], xx_r.at[n], r_x, c)

    d2_tail = send(acct.at[1 - k], d2t, dd_s.at[NCH], dd_r.at[NCH], r_k, c)
    xx_tail = send(xst, xrt, xx_s.at[NCH], xx_r.at[NCH], r_x, c)

    def gather_w():
        with scope("w_in"):
            for rr in range(4):

                @pl.when(r != rr)
                def _():
                    send(wt.at[0:RB], wblk.at[rr], w_s.at[rr], w_r.at[rr], rr, c).wait_recv()

        wf[...] = jnp.concatenate([wblk[rr].astype(F32) for rr in range(4)], axis=1).astype(BF16)

    def close(lo, hi, landed):
        hole = jnp.dot(wf[...], tcol[:, :, lo:hi].reshape(4 * RB, hi - lo), preferred_element_type=F32)
        r1[:, lo:hi] = r1[:, lo:hi] + landed + hole + vo[:, lo:hi].astype(F32)

    def stripe_rows(m):
        return 32 if m < 4 else 16

    def l_copy(m, q):
        there = pl.ds(V * m, stripe_rows(m) * 9 // 2)
        peer = col_peers[q]
        return send(lsnd.at[peer, there], lrcv.at[c, there], l_s.at[m, q], l_r.at[m, q], r, peer)

    def stripe_out(m):
        for n in ((0, 1, 2), (3, 4), (5, 6), (7, 8), (9,))[m]:
            with scope("sum"):
                xx_copy(n).wait_recv()
            close(CW * n, CW * n + CW, xrb[n])
        if m == 4:
            xx_tail.wait_recv()
            close(NCH * CW, CB, xrt[...])
        split_cols(lambda lo, hi: r1[:, lo:hi], planes, m)
        rows = stripe_rows(m)
        for cc in range(4):
            parts = []
            for j in range(4):
                parts += take_j(planes, 4 * cc + j, RB * 8 * m, rows)

            def put_l(at, count, lanes, value):
                lsnd[cc, V * m + at : V * m + at + count, lanes] = value

            pack(put_l, rows, jnp.concatenate(parts, axis=1))
        there = slice(V * m, V * m + rows * 9 // 2)
        lrcv[c, there, :] = lsnd[c, there, :]
        for q in range(3):
            l_copy(m, q).start()

    load_tail.wait()
    part = jnp.dot(tlad[...].reshape(4 * RB, CB), vtail[...], preferred_element_type=F32)
    for rr in range(4):
        acct[rr % 2, rr // 2] = part[RB * rr : RB * rr + RB]
    d2_tail.start()

    def second(n):
        with scope("pair"):
            d2_copy(n).wait_recv()
        xsb[n] = acc[n, k, 1 - x] + d2r[n, 1 - x]
        at = pl.multiple_of(n * CW, CW)
        r1[:, pl.ds(at, CW)] = acc[n, k, x] + d2r[n, x]
        xx_copy(n).start()

    def ladder_step(n, carry):
        slot = n % 2
        with scope("wait_v"):
            load_v(n, slot).wait()
        with scope("dot"):
            for h in range(2):
                part = jnp.dot(
                    tlad[...].reshape(4 * RB, CB), vbuf[slot, :, 256 * h : 256 * h + 256], preferred_element_type=F32
                )
                for rr in range(4):
                    acc[n, rr % 2, rr // 2, :, 256 * h : 256 * h + 256] = part[RB * rr : RB * rr + RB]
        d2_copy(n).start()

        @pl.when(n + 2 < NCH)
        def _():
            load_v(n + 2, slot).start()

        @pl.when(n == 0)
        def _():
            d2_tail.wait_recv()
            xst[...] = acct[k, 1 - x] + d2t[1 - x]
            r1[:, NCH * CW : CB] = acct[k, x] + d2t[x]
            xx_tail.start()

        @pl.when(n > 0)
        def _():
            second(n - 1)

        @pl.when(jnp.logical_and(n == 1, x != z))
        def _():
            for copy in d_copy:
                copy.start()

        @pl.when(jnp.logical_and(n == 1, x == z))
        def _():
            relay(2)

        @pl.when(jnp.logical_and(n == 2, x == z))
        def _():
            relay(3)
            d_copy[2].start()

        @pl.when(jnp.logical_and(n == 3, x == z))
        def _():
            relay(0)

        @pl.when(jnp.logical_and(n == 5, x == z))
        def _():
            relay(1)

        @pl.when(n == jnp.where(x == z, 4, 2))
        def _():
            with scope("hole_w"):
                hole_w()

        @pl.when(jnp.logical_and(n == 9, x != z))
        def _():
            gather_w()
            stripe_out(0)
            stripe_out(1)

        return carry

    lax.fori_loop(0, NCH, ladder_step, 0)
    second(NCH - 1)

    @pl.when(x == z)
    def _():
        gather_w()
        stripe_out(0)
        stripe_out(1)

    def order_rows(src, dst):
        for cc in range(4):
            for i in range(4):
                first = V * i + AB * cc
                for b in range(4):
                    dst[first : first + AB, 128 * b : 128 * b + 128] = src[cc, pl.ds(V * b + i, AB, stride=4), :]
                ends = src[cc, pl.ds(4 * V + i, AB // 2, stride=4), :]
                dst[first : first + AB // 2, 512:576] = ends[:, 0:64]
                dst[first + AB // 2 : first + AB, 512:576] = ends[:, 64:128]

    for m in range(2, 4):
        stripe_out(m)
    order_rows(pt, pp)
    with scope("mirror"):

        @pl.when(jnp.logical_and(x == z, r != c))
        def _():
            p_copy.wait_recv()

        @pl.when(x != z)
        def _():
            for copy in p_on:
                copy.wait_recv()

    order_rows(pr, r3)
    pp[...] = pp[...] + r3[...].T
    for q, peer in enumerate(col_peers):
        with scope("denom"):
            send(dsnd.at[peer], drcv.at[peer], d_s.at[q], d_r.at[q], r, peer).wait_recv()
    order_rows(drcv, r3)
    stripe_out(4)

    for m in range(5):
        rows = stripe_rows(m)
        for q, peer in enumerate(col_peers):
            there = pl.ds(V * m, rows * 9 // 2)
            with scope("regroup"):
                send(
                    lsnd.at[peer, there], lrcv.at[peer, there], l_s.at[m, q], l_r.at[m, q], r, peer
                ).wait_recv()
        for cc in range(4):
            for i in range(4):
                first = V * i + AB * cc + 8 * m
                n = rows // 4

                def finish(at, count, lanes, value):
                    there = slice(at, at + count)
                    out_ref[there, lanes] = (value + pp[there, lanes]) / r3[there, lanes]

                for b in range(4):
                    part = lrcv[cc, pl.ds(V * m + rows * b + i, n, stride=4), :]
                    finish(first, n, slice(128 * b, 128 * b + 128), part)
                ends = lrcv[cc, pl.ds(V * m + 4 * rows + i, n // 2, stride=4), :]
                finish(first, n // 2, slice(512, 576), ends[:, 0:64])
                finish(first + n // 2, n // 2, slice(512, 576), ends[:, 64:128])

    for copy in (col_pair, *q_copy, *d_copy, d2_tail, xx_tail):
        copy.wait_send()
    for m in range(5):
        for q in range(3):
            l_copy(m, q).wait_send()
    for way, h in ((0, 0), (0, 1), (1, 0), (1, 1), (2, 1)):
        row_copy(way, h).wait_send()

    @pl.when(x == z)
    def _():
        row_copy(2, 0).wait_send()
        row_extra.wait_send()
        for h in range(2):
            col_piece(h).wait_send()
        for copy in p_on:
            copy.wait_send()

    @pl.when(jnp.logical_and(x == z, r != c))
    def _():
        p_copy.wait_send()

    @pl.when(x != z)
    def _():
        col_relay.wait_send()
        for copy in p_out:
            copy.wait_send()

    @pl.when(r == c)
    def _():
        for copy in fwd:
            copy.wait_send()

    @pl.when(gives)
    def _():
        for h in range(2):
            for slot in (r_x, r_d):
                lad_forward(slot, h).wait_send()

    for slot in range(4):

        @pl.when(slot != r)
        def _():
            w_copy(slot).wait_send()

        @pl.when(jnp.logical_and(slot != r, jnp.logical_or(slot != c_d, x != z)))
        def _():
            for h in range(2):
                lad_copy(slot, h).wait_send()

    def drain(n, carry):
        d2_copy(n).wait_send()
        xx_copy(n).wait_send()
        return carry

    lax.fori_loop(0, NCH, drain, 0)


def solution(mesh):
    vm = pltpu.VMEM
    dma = pltpu.SemaphoreType.DMA
    scratch = [
        vm((RB, CB), F32), vm((RB, CB), F32), vm((RB, CB), BF16), vm((PB, O * V), BF16),
        vm((4, RB, CB), BF16), vm((4, RB, CB), BF16), vm((4, RB, CB), BF16),
        vm((2, AB * RB, 128), F32), vm((V, O * V), BF16),
        vm((PB, PB), F32), vm((PB, PB), F32), vm((4, PQ, 128), F32), vm((4, PQ, 128), F32),
        vm((4, PQ, 128), F32), vm((4, PQ, 128), F32), vm((4, PQ, 128), F32), vm((4, PQ, 128), F32),
        vm((4, PQ, 128), F32),
        vm((RB, O * O), F32), vm((4, RB, O * O), F32), vm((O * O, RB), BF16), vm((RB, O * O), BF16), vm((4, RB, RB), BF16), vm((RB, O * O), BF16),
        vm((2, CB, CW), BF16), vm((CB, TW), BF16),
        vm((NCH, 2, 2, RB, CW), F32), vm((NCH, 2, RB, CW), F32), vm((NCH, RB, CW), F32), vm((NCH, RB, CW), F32),
        vm((2, 2, RB, TW), F32), vm((2, RB, TW), F32), vm((RB, TW), F32), vm((RB, TW), F32),
        vm((RB, CB), F32),
        dma((6,)), dma((2,)), dma((4, 2)), dma((4, 2)), dma((5,)), dma((5,)), dma((4, 2)), dma((4, 2)),
        dma((3,)), dma((3,)), dma((3,)), dma((3,)), dma((5, 3)), dma((5, 3)), dma((9,)), dma((9,)), dma((4, 2)),
        dma((NCH + 1,)), dma((NCH + 1,)), dma((NCH + 1,)), dma((NCH + 1,)), dma((4,)), dma((4,)), dma((2,)),
    ]
    hbm = pl.BlockSpec(memory_space=pl.ANY)
    vmem = pl.BlockSpec(memory_space=pltpu.VMEM)
    call = pl.pallas_call(
        kernel,
        out_shape=jax.ShapeDtypeStruct((PB, PB), F32),
        in_specs=[hbm] * 6,
        out_specs=vmem,
        scratch_shapes=scratch,
        compiler_params=pltpu.CompilerParams(
            collective_id=0, has_side_effects=True, vmem_limit_bytes=67_000_000
        ),
        name="sweep",
    )
    def local_sweep(t_blk, d_blk, voovv_blk, vvvvv_blk, oooo, w_blk):
        return call(t_blk, d_blk, voovv_blk, vvvvv_blk, oooo, w_blk.T)

    return jax.shard_map(
        local_sweep,
        mesh=mesh,
        in_specs=(P("row", "col"), P("row", "col"), P("row", "col"), P("row", "col"), P(None, None), P(None, "col")),
        out_specs=P("row", "col"),
        check_vma=False,
    )
```

profile of v0, /device:TPU:0, one launch (start us, length us, event | category | flops | bytes accessed | tf_op | source)
XLA Modules:
  0.0 96.2 jit_solution(5981822742039758360)
XLA Ops:
  0.0 93.6 %sweep.1 = f32[576,576]{1,0:T(8,128)} custom-call(f32[64,5184]{1,0:T(8,128)} %t_hbm.1, f32[64,5184]{1,0:T(8,128)} %d_hbm.1, bf16[64,5184]{1,0:T(8,128)(2,1)} %vo_hbm.1, bf16[5184,5184]{1,0:T(8,128)(2,1)} %vv_hbm.1, bf16[256,256]{1,0:T(8,128)(2,1)} %oo_hbm.1, bf16[576,2304]{1,0:T(8,128)(2,1)} %bitcast.1), custom_call_target="tpu_custom_call" | custom-call | tf_op jit(solution)/shard_map/sweep/pallas_call | solution.py:655
  93.6 2.6 %copy.8 = f32[576,576]{1,0:T(8,128)} copy(f32[576,576]{1,0:T(8,128)} %sweep.1) | data formatting | bytes 2654208
where the time goes:
time: 96.5 us; the launch traced here: 96.2 us
  Pallas kernels  93.6 us (97%)
  local copies, waits for them, and re-layouts  2.58 us (3%)
    pallas_call x1, Pallas kernels, local_sweep(): return call(t_blk, d_blk, voovv_blk, vvvvv_blk, oooo, w_blk.T)  93.6 us
    unnamed x1, local copies, waits for them, and re-layouts  2.58 us

commit v1 on v0

--- a/solution.py
+++ b/solution.py
@@ -335,6 +335,7 @@
 
     @pl.when(x == z)
     def _():
+        relay(2)
         with scope("hole_x"):
             hole_x()
 
@@ -469,11 +470,10 @@
 
         @pl.when(jnp.logical_and(n == 1, x == z))
         def _():
-            relay(2)
+            relay(3)
 
         @pl.when(jnp.logical_and(n == 2, x == z))
         def _():
-            relay(3)
             d_copy[2].start()
 
         @pl.when(jnp.logical_and(n == 3, x == z))
@@ -519,6 +519,7 @@
     for m in range(2, 4):
         stripe_out(m)
     order_rows(pt, pp)
+    stripe_out(4)
     with scope("mirror"):
 
         @pl.when(jnp.logical_and(x == z, r != c))
@@ -536,7 +537,6 @@
         with scope("denom"):
             send(dsnd.at[peer], drcv.at[peer], d_s.at[q], d_r.at[q], r, peer).wait_recv()
     order_rows(drcv, r3)
-    stripe_out(4)
 
     for m in range(5):
         rows = stripe_rows(m)

time: 96.5 us -> 92.4 us (0.958)
  Pallas kernels: 93.6 us -> 89.5 us
    pallas_call x1, Pallas kernels: 93.6 us -> 89.5 us  [local_sweep(): return call(t_blk, d_blk, voovv_blk, vvvvv_blk, oooo, w_blk.T)]
where the time goes in v1:
time: 92.4 us; the launch traced here: 92.1 us
  Pallas kernels  89.5 us (97%)
  local copies, waits for them, and re-layouts  2.58 us (3%)
    pallas_call x1, Pallas kernels, local_sweep(): return call(t_blk, d_blk, voovv_blk, vvvvv_blk, oooo, w_blk.T)  89.5 us
    unnamed x1, local copies, waits for them, and re-layouts  2.58 us

profile of v1, /device:TPU:0, one launch (start us, length us, event | category | flops | bytes accessed | tf_op | source)
XLA Modules:
  0.0 92.1 jit_solution(14742059743352542786)
XLA Ops:
  0.0 89.5 %sweep.1 = f32[576,576]{1,0:T(8,128)} custom-call(f32[64,5184]{1,0:T(8,128)} %t_hbm.1, f32[64,5184]{1,0:T(8,128)} %d_hbm.1, bf16[64,5184]{1,0:T(8,128)(2,1)} %vo_hbm.1, bf16[5184,5184]{1,0:T(8,128)(2,1)} %vv_hbm.1, bf16[256,256]{1,0:T(8,128)(2,1)} %oo_hbm.1, bf16[576,2304]{1,0:T(8,128)(2,1)} %bitcast.1), custom_call_target="tpu_custom_call" | custom-call | tf_op jit(solution)/shard_map/sweep/pallas_call | solution.py:655
  89.5 2.6 %copy.8 = f32[576,576]{1,0:T(8,128)} copy(f32[576,576]{1,0:T(8,128)} %sweep.1) | data formatting | bytes 2654208
